TPU v7x, 512 devices: a whole 4x8x8 slice. The times are simulated.
512 devices in a mesh: rep: 8 (over x, y_hi), amp: 64 (over y_lo, z, core).
Axes of the slice: x: 4, y: 8 (y_hi: 2, y_lo: 4; y = y_hi * 4 + y_lo), z: 8, core: 2. Of those that a mesh axis runs over, the one named last changes fastest.
Arguments:
- amplitudes: float32 [2, 16777216], P(None, ('rep', 'amp')), parts along dimension 1, may hold values from -12 to 12
- coupling_index: int32 [16, 20], P('rep'), parts along dimension 0, may hold values from 0 to 15
- rotation_index: int32 [16, 21], P('rep'), parts along dimension 0, may hold values from 0 to 15
- chain_order: int32 [21], replicated, may hold values from 0 to 20, each once
- bond_sign: int32 [20], replicated, may hold values 0 or 1
Outputs:
- final_state: float32 [2, 16777216], P(None, ('rep', 'amp')), parts along dimension 1
- energies: float32 [16], P('rep'), parts along dimension 0
There are 8 independent parts, one for each index of `rep`. A program takes and returns all parts, laid end to end along the dimension named above; an argument that names none is the same for every part. Nothing has to cross between parts.
Inputs may be any that keep to these rules, and one draw needn't show every extreme that they name: chain_order holds each of 0 to 20 once.
All inputs are finite; a program needn't handle non-finite values.
Results may differ from a plain program's by a relative error of at most 0.0003.
Values sent between devices are 32-bit elements; how exact they have to be, the bound alone decides.
No kernel may reach another device: no remote copies, remote signals or barrier semaphores. Data moves between devices by JAX's collectives and lax.ppermute only.
A program may use at most 128 MiB of HBM per device.

v0:
```python
import numpy as np
import jax
import jax.numpy as jnp
from jax import lax
from jax.experimental import pallas as pl
from jax.experimental.pallas import tpu as pltpu
from jax.sharding import PartitionSpec as P

LAYERS = 2
ANGLES = 16
UNITS = 2 * (ANGLES + 1)
LANE_BITS = 7
LANES = 128

F32 = jnp.float32
BF16 = jnp.bfloat16


def angle_tables():
    steps = (np.arange(ANGLES, dtype=np.float64) + 1.0) * (np.pi / UNITS)
    return np.stack([np.cos(steps), np.sin(steps)]).astype(np.float32)


def iota(shape, dimension):
    return lax.broadcasted_iota(jnp.int32, shape, dimension)


def bit_count(values, width):
    total = values & 1
    for bit in range(1, width):
        total = total + ((values >> bit) & 1)
    return total


def split(values):
    high = values.astype(BF16)
    return high, (values - high.astype(F32)).astype(BF16)


def dot(left, right):
    return jnp.dot(left, right, preferred_element_type=F32)


def product(left, right):
    return dot(
        jnp.concatenate([left[0], left[0], left[1]], axis=1),
        jnp.concatenate([right[0], right[1], right[0]], axis=0),
    )


SWAPS = 4
ROWQ, LANEQ, SWAPPED, LATE, SPARE, PLAN = 0, 8, 12, 13, 14, 16


def gate(bits, width):
    column = iota((1, width), 1)
    lines = []
    for place, cosine, sine in bits:
        one = ((column >> place) & 1) == 1
        lines.append((jnp.where(one, sine, cosine), jnp.where(one, cosine, -sine)))
    row = iota((8, width), 0)
    matrix = None
    for bit, (zero_line, one_line) in enumerate(lines[:3]):
        factor = jnp.where(((row >> bit) & 1) == 1, one_line, zero_line)
        matrix = factor if matrix is None else matrix * factor
    for zero_line, one_line in lines[3:]:
        matrix = jnp.concatenate([matrix * zero_line, matrix * one_line], axis=0)
    return matrix


def lane_bits(pairs):
    return [(place, cosine, -sine) for place, (cosine, sine) in enumerate(pairs)]


def pair_of(layer, rotation_ref, table_ref, qubit, keep=None):
    index = rotation_ref[layer, qubit]
    cosine, sine = table_ref[0, index], table_ref[1, index]
    if keep is None:
        return cosine, sine
    return jnp.where(keep, cosine, F32(1.0)), jnp.where(keep, sine, F32(0.0))


def cos_sin(steps):
    quarter = UNITS // 2
    turns = jnp.floor(steps * (1.0 / quarter) + 0.5)
    angle = (steps - turns * quarter) * (np.pi / UNITS)
    square = angle * angle
    sine = angle * (
        1.0 + square * (-1.0 / 6 + square * (1.0 / 120 + square * (-1.0 / 5040 + square * (1.0 / 362880))))
    )
    cosine = 1.0 + square * (
        -0.5 + square * (1.0 / 24 + square * (-1.0 / 720 + square * (1.0 / 40320)))
    )
    turns = turns.astype(jnp.int32)
    odd = (turns & 1) == 1
    cosine, sine = jnp.where(odd, sine, cosine), jnp.where(odd, cosine, sine)
    return (
        jnp.where(((turns + 1) & 2) == 2, -cosine, cosine),
        jnp.where((turns & 2) == 2, -sine, sine),
    )


def looked_up(steps):
    period = 2 * UNITS
    place = (steps - period * jnp.floor(steps * (1.0 / period) + 0.25 / period)).astype(jnp.int32)
    cosine, sine = cos_sin(iota((8, LANES), 1).astype(F32))
    tiles = place.reshape(-1, 8, LANES)
    pick = lambda table: jnp.concatenate(
        [jnp.take_along_axis(table, tiles[k], axis=1, mode="promise_in_bounds") for k in range(tiles.shape[0])],
        axis=0,
    )
    return pick(cosine), pick(sine)


def turned(cosine, sine, real, imag):
    return cosine * real + sine * imag, cosine * imag - sine * real


def sign_rows(start, first, low, high, line):
    row = iota((8, start.shape[1]), 0)
    rows = jnp.broadcast_to(start, row.shape)
    for bit in range(low):
        rows = jnp.where(((row >> bit) & 1) == 1, rows * line(first + bit), rows)
    for bit in range(low, low + high):
        rows = jnp.concatenate([rows, rows * line(first + bit)], axis=0)
    return rows


def flips(positions, bonds):
    first, second = positions[:, 0:bonds], positions[:, 1 : bonds + 1]
    return lambda bit: jnp.where((first == bit) | (second == bit), F32(-1.0), F32(1.0))


def lane_part(positions, bonds):
    ones = jnp.ones((1, bonds), F32)
    return sign_rows(ones, 0, 3, LANE_BITS - 3, flips(positions, bonds)).astype(BF16)


def fields(weights, positions, lanes, device_bits, bonds, row_bits):
    differ = (device_bits >> positions[:, 0:bonds]) ^ (device_bits >> positions[:, 1 : bonds + 1])
    device_sign = (1 - 2 * (differ & 1)).astype(F32)
    line = flips(positions, bonds)
    stacked = jnp.concatenate(
        [sign_rows(w * device_sign, LANE_BITS, 3, row_bits - 3, line).astype(BF16) for w in weights],
        axis=0,
    )
    out = lax.dot_general(
        stacked, lanes, (((1,), (1,)), ((), ())), preferred_element_type=F32
    )
    rows = 2**row_bits
    return [out[k * rows : (k + 1) * rows] for k in range(len(weights))]


def energy(real, imag, field):
    return jnp.sum((real * real + imag * imag) * field)


def in_lanes(parts):
    lane = iota((1, LANES), 1)
    row = jnp.zeros((1, LANES), F32)
    for k, part in enumerate(parts):
        row = jnp.where(lane == k, part, row)
    return row


def evens(ref):
    half = ref.shape[0] // 2
    return ref[pl.ds(0, half, stride=2), :], ref[pl.ds(1, half, stride=2), :]


def take_blocks(ref, blocks, height, kept):
    def part(component):
        return jnp.concatenate(
            [ref[pl.ds(2 * k + component, blocks, stride=height), :] for k in range(kept)], axis=0
        )

    return part(0), part(1)


def put_blocks(ref, blocks, height, kept, real, imag):
    for k in range(kept):
        here = slice(k * blocks, (k + 1) * blocks)
        ref[pl.ds(2 * k, blocks, stride=height), :] = real[here]
        ref[pl.ds(2 * k + 1, blocks, stride=height), :] = imag[here]


def by_rows(gates, real, imag):
    both = product(gates, split(jnp.concatenate([real, imag], axis=1)))
    return both[:, :LANES], both[:, LANES:]


def by_blocks(gates, real, imag):
    size = gates[0].shape[0]
    pieces = [p[k : k + size] for p in (real, imag) for k in range(0, real.shape[0], size)]
    out = product(gates, split(jnp.concatenate(pieces, axis=1)))
    pieces = [out[:, k * LANES : (k + 1) * LANES] for k in range(len(pieces))]
    half = len(pieces) // 2
    return jnp.concatenate(pieces[:half], axis=0), jnp.concatenate(pieces[half:], axis=0)


def by_lanes(gates, real, imag):
    rows = real.shape[0]
    both = product(split(jnp.concatenate([real, imag], axis=0)), gates)
    return both[:rows], both[rows:]


def swap(buffer, plan_ref, slots):
    for i in range(SWAPS):
        @pl.when(i < plan_ref[0, SWAPPED])
        def _(i=i):
            height = 2 ** (slots - 1 - i)
            place = plan_ref[0, LANEQ + i]
            step = jnp.left_shift(jnp.int32(1), place)
            if height == 4:
                tiles = buffer[...].reshape(-1, 8, LANES)
                other = pltpu.roll(tiles, 4, 1)
                one = (iota((1, 8, LANES), 2) >> place) & 1
                same = one == (iota((1, 8, LANES), 1) >> 2)
                moved = jnp.where(one == 1, pltpu.roll(other, step, 2), pltpu.roll(other, LANES - step, 2))
                buffer[...] = jnp.where(same, tiles, moved).reshape(buffer.shape)
                return
            whole = buffer[...].reshape(-1, 2, height, LANES)
            low, high = whole[:, 0].reshape(-1, LANES), whole[:, 1].reshape(-1, LANES)
            one = ((iota((1, LANES), 1) >> place) & 1) == 1
            new_low = jnp.where(one, pltpu.roll(high, step, 1), low)
            new_high = jnp.where(one, high, pltpu.roll(low, LANES - step, 1))
            pairs = (new_low.reshape(-1, 1, height, LANES), new_high.reshape(-1, 1, height, LANES))
            buffer[...] = jnp.concatenate(pairs, axis=1).reshape(buffer.shape)


class Plan:
    def __init__(self, local_bits, global_bits):
        self.local_bits, self.global_bits = local_bits, global_bits
        self.qubits = local_bits + global_bits
        self.row_bits = local_bits - LANE_BITS
        self.rows = 2**self.row_bits
        self.blocks = 2**global_bits
        self.kept_bits = self.row_bits - global_bits
        self.kept = 2**self.kept_bits
        self.bonds = self.qubits - 1


def choose(plan, chain_ref, plan_ref):
    order = [chain_ref[0, k] for k in range(plan.qubits)]
    away = [(q >= plan.local_bits).astype(jnp.int32) for q in order]
    free = jnp.int32(0)
    for k, q in enumerate(order):
        near = away[k]
        if k:
            near = near | away[k - 1]
        if k + 1 < plan.qubits:
            near = near | away[k + 1]
        free = free | jnp.left_shift(1 - near, q)
    bit = lambda q: (free >> q) & 1
    row_qubits = range(LANE_BITS, plan.local_bits)
    free_rows = sum(bit(q) for q in row_qubits)
    slots = plan.global_bits
    free_lanes = sum(bit(q) for q in range(LANE_BITS))
    swapped = jnp.minimum(jnp.minimum(free_lanes, SWAPS), jnp.maximum(slots - free_rows, 0))
    late = jnp.maximum(slots - swapped - free_rows, 0)
    seen = jnp.int32(0)
    for k, q in enumerate(row_qubits):
        held = k - seen
        rank = jnp.where(bit(q) == 1, late + seen, jnp.where(held < late, held, free_rows + held))
        plan_ref[0, ROWQ + rank] = jnp.int32(q)
        seen = seen + bit(q)
    for i in range(SWAPS):
        plan_ref[0, LANEQ + i] = jnp.int32(-1)
    seen = jnp.int32(0)
    for q in range(LANE_BITS):
        taken = (bit(q) == 1) & (seen < swapped)
        plan_ref[0, jnp.where(taken, LANEQ + seen, SPARE)] = jnp.int32(q)
        seen = seen + bit(q)
    plan_ref[0, SWAPPED] = swapped
    plan_ref[0, LATE] = late


def touches(plan, chain, plan_ref, rows_from, rows_to, lanes):
    hit = jnp.zeros(chain.shape, jnp.int32)
    for b in range(plan.global_bits):
        wanted = (b >= rows_from) & (b < rows_to)
        hit = hit | (chain == jnp.where(wanted, plan_ref[0, ROWQ + b], -1)).astype(jnp.int32)
    if lanes:
        for i in range(SWAPS):
            hit = hit | (chain == plan_ref[0, LANEQ + i]).astype(jnp.int32)
    return (hit[:, 0 : plan.bonds] | hit[:, 1 : plan.bonds + 1]).astype(F32)


def ordered_positions(plan, chain, plan_ref):
    places = chain
    for b in range(plan.row_bits):
        places = jnp.where(chain == plan_ref[0, ROWQ + b], LANE_BITS + b, places)
    return places


def moved_positions(plan, chain, plan_ref):
    slots, swapped = plan.global_bits, plan_ref[0, SWAPPED]
    places = jnp.where(chain >= plan.local_bits, chain - plan.local_bits + LANE_BITS, chain)
    for b in range(plan.row_bits):
        target = jnp.int32(LANE_BITS + b)
        if b < slots:
            target = jnp.int32(plan.local_bits + b)
            i = slots - 1 - b
            if i < SWAPS:
                target = jnp.where(i < swapped, plan_ref[0, LANEQ + i], target)
        places = jnp.where(chain == plan_ref[0, ROWQ + b], target, places)
    for i in range(SWAPS):
        places = jnp.where(chain == plan_ref[0, LANEQ + i], plan.local_bits + slots - 1 - i, places)
    return places


def row_ones(plan, device):
    tile = bit_count(iota((8, LANES), 0), 3) + bit_count(iota((8, LANES), 1), LANE_BITS)
    tile = tile + bit_count(device, plan.global_bits)
    return jnp.concatenate([tile + k.bit_count() for k in range(plan.rows // 8)], axis=0)


def first_kernel(
    plan, rotation_ref, table_ref, order_ref, chain_ref, coupling_ref, bond_ref, amps_ref,
    out_ref, sums_ref, plan_ref, buffer,
):
    device = lax.axis_index("amp")
    bonds, rows = plan.bonds, plan.rows
    choose(plan, order_ref, plan_ref)
    chain = chain_ref[...]
    device_bits = device << plan.local_bits
    bond_signs = (2 * bond_ref[...] - 1).astype(F32)
    lanes = lane_part(chain, bonds)
    (steps,) = fields(
        [(coupling_ref[0:1, :] + 1).astype(F32) * bond_signs],
        chain, lanes, device_bits, bonds, plan.row_bits,
    )
    steps = steps + (UNITS // 2) * row_ones(plan, device).astype(F32)
    pair = lambda layer, q, keep=None: pair_of(layer, rotation_ref, table_ref, q, keep)

    real, imag = evens(amps_ref)
    norm = jnp.sum(real * real + imag * imag)
    real, imag = turned(*looked_up(steps), real, imag)
    ranked = [plan_ref[0, ROWQ + b] for b in range(plan.row_bits)]
    row_gate = gate([(q - LANE_BITS, *pair(0, q)) for q in ranked], rows)
    lane_gate = gate(lane_bits([pair(0, q) for q in range(LANE_BITS)]), LANES)
    real, imag = by_rows(split(row_gate), real, imag)
    real, imag = by_lanes(split(lane_gate), real, imag)

    late, slots = plan_ref[0, LATE], plan.global_bits - plan_ref[0, SWAPPED]
    early = touches(plan, chain, plan_ref, late, slots, True)
    weight = early * bond_signs
    steps, signs = fields(
        [(coupling_ref[1:2, :] + 1).astype(F32) * weight, weight],
        ordered_positions(plan, chain, plan_ref), lanes, device_bits, bonds, plan.row_bits,
    )
    sums_ref[...] = in_lanes([norm, energy(real, imag, signs)])
    real, imag = turned(*looked_up(steps), real, imag)
    bits = []
    for b in range(plan.global_bits):
        bits.append((b, *pair(1, ranked[b], (b >= late) & (b < slots))))
    real, imag = by_blocks(split(gate(bits, plan.blocks)), real, imag)
    pairs = []
    for q in range(LANE_BITS):
        keep = q == plan_ref[0, LANEQ]
        for i in range(1, SWAPS):
            keep = keep | (q == plan_ref[0, LANEQ + i])
        pairs.append(pair(1, q, keep))
    real, imag = by_lanes(split(gate(lane_bits(pairs), LANES)), real, imag)
    buffer[...] = jnp.concatenate([real, imag], axis=0)
    swap(buffer, plan_ref, plan.global_bits)
    put_blocks(out_ref, plan.blocks, 2 * plan.kept, plan.kept, buffer[:rows], buffer[rows:])


def prepare_kernel(
    plan, rotation_ref, table_ref, plan_ref, chain_ref, coupling_ref, bond_ref,
    mode_ref, cosine_ref, sine_ref, before_ref, after_ref, late_ref, turn_ref, *gate_refs,
):
    late_rows = plan_ref[0, LATE]
    mode_ref[0, 0] = jnp.minimum(late_rows, 2)
    device = lax.axis_index("amp")
    bonds, rows, slots = plan.bonds, plan.rows, plan.global_bits
    chain = chain_ref[...]
    bond_signs = (2 * bond_ref[...] - 1).astype(F32)
    rest = bond_signs * (1.0 - touches(plan, chain, plan_ref, late_rows, slots - plan_ref[0, SWAPPED], True))
    after_trade = jnp.where(late_rows >= 2, late_rows, 0)
    late = bond_signs * touches(plan, chain, plan_ref, 0, after_trade, False)
    moved = moved_positions(plan, chain, plan_ref)
    device_bits = device << plan.local_bits
    steps, before_ref[...], after_ref[...] = fields(
        [(coupling_ref[1:2, :] + 1).astype(F32) * rest, rest, bond_signs - late],
        moved, lane_part(moved, bonds), device_bits, bonds, plan.row_bits,
    )
    cosine_ref[...], sine_ref[...] = looked_up(steps)
    (late_ref[...],) = fields([late], chain, lane_part(chain, bonds), device_bits, bonds, plan.row_bits)
    pair = lambda layer, q, keep=None: pair_of(layer, rotation_ref, table_ref, q, keep)
    ranked = [plan_ref[0, ROWQ + b] for b in range(plan.row_bits)]
    cosine, sine = pair(1, ranked[0])
    turn_ref[...] = in_lanes([cosine, jnp.where((device & 1) == 1, -sine, sine)])
    far = [plan.local_bits + b for b in range(slots)]
    lane_pairs = []
    for q in range(LANE_BITS):
        held = jnp.int32(q)
        for i in range(SWAPS):
            held = jnp.where(plan_ref[0, LANEQ + i] == q, ranked[slots - 1 - i], held)
        lane_pairs.append(pair(1, held))
    back = []
    for b in range(plan.row_bits):
        cosine, sine = pair(1, ranked[b], b < after_trade)
        back.append((ranked[b] - LANE_BITS, cosine, -sine))
    gates = [
        gate([(b, *pair(0, q)) for b, q in enumerate(far)], plan.blocks),
        gate([(b, *pair(1, q)) for b, q in enumerate(far + ranked[slots:])], rows),
        gate(lane_bits(lane_pairs), LANES),
        gate(back, rows).T,
    ]
    for k, made in enumerate(gates):
        gate_refs[2 * k][...], gate_refs[2 * k + 1][...] = split(made)


def middle(plan, state_ref, cosine_ref, sine_ref, before_ref, gates):
    ga, gb, ha, hb, la, lb = gates
    real, imag = take_blocks(state_ref, plan.blocks, 2 * plan.kept, plan.kept)
    real, imag = by_blocks((ga[...], gb[...]), real, imag)
    before = energy(real, imag, before_ref[...])
    real, imag = turned(cosine_ref[...], sine_ref[...], real, imag)
    real, imag = by_rows((ha[...], hb[...]), real, imag)
    return *by_lanes((la[...], lb[...]), real, imag), before


def pack(plan, out_ref, real, imag, sums):
    blocks, kept = plan.blocks, plan.kept
    height = 2 * kept + 1
    put_blocks(out_ref, blocks, height, kept, real, imag)
    out_ref[pl.ds(2 * kept, blocks, stride=height), :] = jnp.broadcast_to(sums, (blocks, LANES))


def middle_kernel(plan, state_ref, cosine_ref, sine_ref, before_ref, after_ref, sums_ref, *refs):
    real, imag, before = middle(plan, state_ref, cosine_ref, sine_ref, before_ref, refs[:6])
    after = energy(real, imag, after_ref[...])
    pack(plan, refs[6], real, imag, sums_ref[...] + in_lanes([F32(0.0), before, after]))


def open_kernel(plan, state_ref, cosine_ref, sine_ref, before_ref, sums_ref, *refs):
    gates, (out_ref, sums_out_ref) = refs[:6], refs[6:]
    real, imag, before = middle(plan, state_ref, cosine_ref, sine_ref, before_ref, gates)
    out_ref[...] = jnp.concatenate([real, imag], axis=0)
    sums_out_ref[...] = sums_ref[...] + in_lanes([F32(0.0), before])


def close_kernel(plan, own_ref, other_ref, turn_ref, after_ref, sums_ref, out_ref):
    both = turn_ref[0:1, 0:1] * own_ref[...] + turn_ref[0:1, 1:2] * other_ref[...]
    real, imag = both[: plan.rows], both[plan.rows :]
    after = energy(real, imag, after_ref[...])
    pack(plan, out_ref, real, imag, sums_ref[...] + in_lanes([F32(0.0), F32(0.0), after]))


def last_kernel(plan, plan_ref, state_ref, ga, gb, *refs):
    late_ref, (out_ref, energies_ref, *late_out_ref, buffer) = refs[:-3][:1], refs[-4 if len(refs) == 5 else -3 :]
    device = lax.axis_index("amp")
    blocks, kept, rows = plan.blocks, plan.kept, plan.rows
    height = 2 * kept + 1
    sums = jnp.sum(state_ref[pl.ds(2 * kept, blocks, stride=height), :], axis=0, keepdims=True)
    amps = float(2**plan.qubits)
    mean = sums[:, 0:1] / amps + 1e-06
    factor = 1.0 / jnp.sqrt(mean)
    square = factor * factor / amps
    energies_ref[...] = sums[:, 1 : 1 + LAYERS] * square
    real, imag = take_blocks(state_ref, blocks, height, kept)
    buffer[...] = jnp.concatenate([real, imag], axis=0)
    swap(buffer, plan_ref, plan.global_bits)
    real, imag = by_rows((ga[...], gb[...]), buffer[:rows], buffer[rows:])
    if late_ref:
        late_out_ref[0][...] = in_lanes([0.0, energy(real, imag, late_ref[0][...])])[:, 0:LAYERS] * square
    ones = row_ones(plan, device)
    odd = (ones & 1) == 1
    real, imag = jnp.where(odd, imag, real), jnp.where(odd, real, imag)
    real = jnp.where(((ones + 1) & 2) == 2, -factor, factor) * real
    imag = jnp.where((ones & 2) == 2, -factor, factor) * imag
    out_ref[pl.ds(0, rows, stride=2), :] = real
    out_ref[pl.ds(1, rows, stride=2), :] = imag


def spec(space):
    return pl.BlockSpec(memory_space=space)


def call(kernel, shapes, scalars, arrays, name, spaces=None, scratch=(), near=0, held=(), far=(), plan=None):
    kept = len(arrays) - near
    arrays = tuple(
        pltpu.with_memory_space_constraint(a, pltpu.VMEM) if k >= kept else a
        for k, a in enumerate(arrays)
    )
    if plan is not None:
        scalars = (*scalars, pltpu.with_memory_space_constraint(plan, pltpu.SMEM))
    spaces = spaces or (pltpu.VMEM,) * len(shapes)
    shapes = tuple(
        spaces[k](s.shape, s.dtype) if k in held else pltpu.HBM(s.shape, s.dtype) if k in far else s
        for k, s in enumerate(shapes)
    )
    return pl.pallas_call(
        kernel,
        out_shape=shapes,
        in_specs=[spec(pltpu.SMEM)] * len(scalars) + [spec(pltpu.VMEM)] * len(arrays),
        out_specs=tuple(spec(s) for s in spaces),
        scratch_shapes=scratch,
        name=name,
    )(*scalars, *arrays)


def local(amplitudes, coupling_index, rotation_index, chain_order, bond_sign):
    local_bits = amplitudes.shape[1].bit_length() - 1
    size = lax.axis_size("amp")
    plan = Plan(local_bits, size.bit_length() - 1)
    rows = plan.rows
    shape = jax.ShapeDtypeStruct
    bind = lambda kernel: lambda *refs: kernel(plan, *refs)

    state = amplitudes.reshape(2, rows, LANES).transpose(1, 0, 2).reshape(2 * rows, LANES)
    table = jnp.asarray(angle_tables())
    chain, bond = chain_order.reshape(1, -1), bond_sign.reshape(1, -1)
    small = (chain, coupling_index, bond)
    whole = shape((2 * rows, LANES), F32)
    field, line = shape((rows, LANES), F32), shape((1, LANES), F32)
    square_of = lambda n: shape((n, n), BF16)
    buffer = (pltpu.VMEM((2 * rows, LANES), F32),)

    state, sums, chosen = call(
        bind(first_kernel),
        (whole, line, shape((1, PLAN), jnp.int32)),
        (rotation_index, table, chain), (*small, state), "first",
        (pltpu.VMEM, pltpu.VMEM, pltpu.SMEM), buffer, held=(0, 1, 2),
    )
    sizes = (size, rows, LANES, rows)
    made = call(
        bind(prepare_kernel),
        (shape((1, 1), jnp.int32),) + (field,) * 5 + (line,)
        + tuple(square_of(n) for n in sizes for _ in range(2)),
        (rotation_index, table), small, "prepare",
        (pltpu.SMEM,) + (pltpu.VMEM,) * 14, held=range(1, 15), plan=chosen,
    )
    mode, fields_made, late, turn, gates = made[0], made[1:5], made[5], made[6], made[7:]
    state = lax.all_to_all(state.reshape(size, 2 * plan.kept, LANES), "amp", 0, 0, tiled=True)
    state = state.reshape(2 * rows, LANES)
    height = 2 * plan.kept + 1
    pair = shape((1, LAYERS), F32)

    packed = (shape((size * height, LANES), F32),)

    def straight(state, sums, turn, made):
        return call(
            bind(middle_kernel), packed, (), (state, *made[:4], sums, *made[4:10]),
            "middle", near=12, held=(0,),
        )

    def paired(state, sums, turn, made):
        own, sums = call(
            bind(open_kernel), (whole, line), (),
            (state, *made[:3], sums, *made[4:10]), "open", near=11, held=(0, 1),
        )
        other = lax.ppermute(own, "amp", [(k, k ^ 1) for k in range(size)])
        return call(
            bind(close_kernel), packed, (),
            (own, other, turn, made[3], sums), "close", near=5, held=(0,),
        )

    def end(middle_of, state, sums, turn, chosen, made, *late):
        (state,) = middle_of(state, sums, turn, made)
        state = lax.all_to_all(state.reshape(size, height, 1, LANES), "amp", 0, 0, tiled=True)
        return call(
            bind(last_kernel), (whole, pair) + (pair,) * len(late), (),
            (state.reshape(size * height, LANES), *made[10:], *late), "last",
            scratch=buffer, near=3 + len(late), far=() if late else (0, 1), plan=chosen,
        )

    def apart(final):
        return final.reshape(rows, 2, LANES).transpose(1, 0, 2).reshape(2, rows * LANES)

    def none_late(*operands):
        final, energies = end(straight, *operands[:-1])
        return apart(final), energies.reshape(LAYERS)

    def one_late(*operands):
        final, energies = end(paired, *operands[:-1])
        return apart(final), energies.reshape(LAYERS)

    def more_late(*operands):
        final, energies, extra = end(straight, *operands)
        sent = jnp.broadcast_to(extra[None], (size, 1, LAYERS))
        total = energies + lax.all_to_all(sent, "amp", 0, 0, tiled=True).sum(axis=0)
        return apart(final), total.reshape(LAYERS)

    return lax.switch(
        mode[0, 0], (none_late, one_late, more_late),
        state, sums, turn, chosen, (*fields_made, *gates), late,
    )


def solution(mesh):
    in_specs = (P(None, ("rep", "amp")), P("rep", None), P("rep", None), P(), P())
    out_specs = (P(None, ("rep", "amp")), P("rep"))
    return jax.shard_map(local, mesh=mesh, in_specs=in_specs, out_specs=out_specs, check_vma=False)
```

profile of v0, /device:TPU:1, one launch (start us, length us, event | category | flops | bytes accessed | tf_op | source)
XLA Modules:
  0.0 51.7 jit_solution(12541063192898468946)
XLA Ops:
  0.6 3.6 %first.1 = (f32[512,128]{1,0:T(8,128)}, f32[1,128]{1,0:T(1,128)S(1)}, s32[1,16]{1,0:T(1,128)S(4)}) custom-call(s32[2,21]{1,0:T(2,128)} %refs_0_.3, f32[2,16]{1,0:T(2,128)} %constant.10.clone.refs_1_, s32[1,21]{1,0:T(1,128)} %bitcast.45, s32[1,21]{1,0:T(1,128)} %bitcast.46, s32[2,20]{1,0:T(2,128)} %refs_4_.3, s32[1,20]{1,0:T(1,128)} %bitcast.48, ...), custom_call_target="tpu_custom_call" | custom-call | tf_op jit(solution)/shard_map/first/pallas_call | solution.py:496
  4.3 15.4 %all-to-all-start.4 = ((f32[64,8,128]{2,1,0:T(8,128)}), f32[64,8,128]{2,1,0:T(8,128)S(1)}, u32[]{:S(2)}, u32[]{:S(2)}) async-start(f32[64,8,128]{2,1,0:T(8,128)} %bitcast.29), calls=%async_computation.4 | async-start | bytes 524288 | tf_op jit(solution)/shard_map/all_to_all | solution.py:538
  19.7 1.7 %prepare.1 = (s32[1,1]{1,0:T(1,128)}, f32[256,128]{1,0:T(8,128)S(1)}, f32[256,128]{1,0:T(8,128)S(1)}, f32[256,128]{1,0:T(8,128)S(1)}, f32[256,128]{1,0:T(8,128)S...) custom-call(s32[2,21]{1,0:T(2,128)} %refs_0_.3, ...), custom_call_target="tpu_custom_call" | custom-call | tf_op jit(solution)/shard_map/prepare/pallas_call | solution.py:496
  22.0 9.2 %all-to-all-done.4 = f32[64,8,128]{2,1,0:T(8,128)S(1)} async-done(((f32[64,8,128]{2,1,0:T(8,128)}), f32[64,8,128]{2,1,0:T(8,128)S(1)}, u32[]{:S(2)}, u32[]{:S(2)}) %all-to-all-start.4) | async-done | bytes 262176 | tf_op jit(solution)/shard_map/all_to_all | solution.py:538
  31.2 20.5 %conditional.1 = (f32[1,2]{1,0:T(1,128)}, f32[2,32768]{1,0:T(2,128)}) conditional(s32[]{:T(128)} %bitcast.28, (f32[512,128]{1,0:T(8,128)S(1)}, f32[256,128]{1,0:T(8,128)S(1)}, f32[256,128]{1,0:T(8,128)S(1)}, f32[256,128]{1,0:T(8,128)S(1)}, f32[256,128]{1,0:T(8,128)S(1)}, /*index=5*/f32[1,128]{1,0:T(1,128)S(1)}, ...), branch_computations={%region_0.0_spmd, %region_1.0_spmd, %region_2.0_spmd} | conditional | flops 128 | bytes 1638456 | solution.py:588
  31.2 1.0 %middle.2 = f32[576,128]{1,0:T(8,128)S(1)} custom-call(f32[512,128]{1,0:T(8,128)S(1)} %get-tuple-element.95.refs_0_, f32[256,128]{1,0:T(8,128)S(1)} %get-tuple-element.96.refs_1_, f32[256,128]{1,0:T(8,128)S(1)} %get-tuple-element.97.refs_2_, f32[256,128]{1,0:T(8,128)S(1)} %get-tuple-element.98.refs_3_, f32[256,128]{1,0:T(8,128)S(1)} %get-tuple-element.99.refs_4_, ...), custom_call_target="tpu_custom_call" | custom-call | tf_op jit(solution)/shard_map/cond/branch_0_fun/middle/pallas_call | solution.py:496
  32.2 18.0 %all_to_all.21 = f32[64,9,1,128]{3,2,1,0:T(1,128)S(1)} all-to-all(f32[64,9,1,128]{3,2,1,0:T(1,128)S(1)} %bitcast.42), channel_id=1, replica_groups=mesh['rep'=8,'amp'=64] {'amp'}, dimensions={0} | all-to-all | bytes 589824 | tf_op jit(solution)/shard_map/cond/branch_0_fun/all_to_all | solution.py:564
  50.2 1.4 %last.3 = (f32[512,128]{1,0:T(8,128)}, f32[1,2]{1,0:T(1,128)}) custom-call(s32[1,16]{1,0:T(1,128)S(4)} %get-tuple-element.94.refs_0_, f32[576,128]{1,0:T(8,128)S(1)} %bitcast.38, bf16[256,256]{1,0:T(8,128)(2,1)S(1)} %get-tuple-element.107.refs_2_, bf16[256,256]{1,0:T(8,128)(2,1)S(1)} %get-tuple-element.108.refs_3_), custom_call_target="tpu_custom_call" | custom-call | tf_op jit(solution)/shard_map/cond/branch_0_fun/last/pallas_call | solution.py:496
Async XLA Ops:
  4.3 26.9 %all-to-all-start.4 = ((f32[64,8,128]{2,1,0:T(8,128)}), f32[64,8,128]{2,1,0:T(8,128)S(1)}, u32[]{:S(2)}, u32[]{:S(2)}) async-start(f32[64,8,128]{2,1,0:T(8,128)} %bitcast.29), calls=%async_computation.4 | async-start | bytes 524288 | tf_op jit(solution)/shard_map/all_to_all | solution.py:538
where the time goes:
time: 51.9 us; the launch traced here: 51.7 us
  blocking collectives  18 us (35%)
  starting transfers between devices  15.4 us (30%)
  waiting for transfers between devices  9.2 us (18%)
  Pallas kernels  7.73 us (15%)
  between operations  1.3 us (3%)
    all_to_all x1, blocking collectives, end(): lax.all_to_all(state.reshape(size, height, 1, LANES), 'amp', 0, 0, tiled=...  18 us
    all_to_all x1, starting transfers between devices, local(): lax.all_to_all(state.reshape(size, 2 * plan.kept, LANES), 'amp', 0, 0, ti...  15.4 us
    all_to_all x1, waiting for transfers between devices, local(): lax.all_to_all(state.reshape(size, 2 * plan.kept, LANES), 'amp', 0, 0, ti...  9.2 us
    pallas_call x4, Pallas kernels, call(): pl.pallas_call(kernel, out_shape=shapes, in_specs=[spec(pltpu.SMEM)] * le...  7.73 us
  transfers between devices with their start and end apart: 1, of which 1 were waited for; matrix products, arithmetic and copies ran while one was open for 0% of the time, Pallas kernels for 3%

commit v1 on v0

--- a/solution.py
+++ b/solution.py
@@ -204,6 +204,17 @@
     return both[:rows], both[rows:]
 
 
+def across(values, step):
+    place = iota((8, LANES), 1) ^ step
+    return jnp.concatenate(
+        [
+            jnp.take_along_axis(values[k : k + 8], place, axis=1, mode="promise_in_bounds")
+            for k in range(0, values.shape[0], 8)
+        ],
+        axis=0,
+    )
+
+
 def swap(buffer, plan_ref, slots):
     for i in range(SWAPS):
         @pl.when(i < plan_ref[0, SWAPPED])
@@ -216,14 +227,14 @@
                 other = pltpu.roll(tiles, 4, 1)
                 one = (iota((1, 8, LANES), 2) >> place) & 1
                 same = one == (iota((1, 8, LANES), 1) >> 2)
-                moved = jnp.where(one == 1, pltpu.roll(other, step, 2), pltpu.roll(other, LANES - step, 2))
+                moved = across(other.reshape(-1, LANES), step).reshape(tiles.shape)
                 buffer[...] = jnp.where(same, tiles, moved).reshape(buffer.shape)
                 return
             whole = buffer[...].reshape(-1, 2, height, LANES)
             low, high = whole[:, 0].reshape(-1, LANES), whole[:, 1].reshape(-1, LANES)
             one = ((iota((1, LANES), 1) >> place) & 1) == 1
-            new_low = jnp.where(one, pltpu.roll(high, step, 1), low)
-            new_high = jnp.where(one, high, pltpu.roll(low, LANES - step, 1))
+            crossed = across(jnp.where(one, low, high), step)
+            new_low, new_high = jnp.where(one, crossed, low), jnp.where(one, high, crossed)
             pairs = (new_low.reshape(-1, 1, height, LANES), new_high.reshape(-1, 1, height, LANES))
             buffer[...] = jnp.concatenate(pairs, axis=1).reshape(buffer.shape)
 
@@ -315,10 +326,18 @@
     return jnp.concatenate([tile + k.bit_count() for k in range(plan.rows // 8)], axis=0)
 
 
-def first_kernel(
-    plan, rotation_ref, table_ref, order_ref, chain_ref, coupling_ref, bond_ref, amps_ref,
-    out_ref, sums_ref, plan_ref, buffer,
-):
+def first_kernel(plan, *refs):
+    sources, (out_ref, sums_ref, plan_ref, buffer), held = refs[:6], refs[6:10], refs[10:16]
+    table_ref, semaphores = refs[16:]
+    copies = [pltpu.make_async_copy(s, h, semaphores.at[k]) for k, (s, h) in enumerate(zip(sources, held))]
+    for copy in copies:
+        copy.start()
+    for k, values in enumerate(angle_tables()):
+        for at, value in enumerate(values):
+            table_ref[k, at] = F32(value)
+    for copy in copies[:-1]:
+        copy.wait()
+    rotation_ref, order_ref, chain_ref, coupling_ref, bond_ref, amps_ref = held
     device = lax.axis_index("amp")
     bonds, rows = plan.bonds, plan.rows
     choose(plan, order_ref, plan_ref)
@@ -333,6 +352,7 @@
     steps = steps + (UNITS // 2) * row_ones(plan, device).astype(F32)
     pair = lambda layer, q, keep=None: pair_of(layer, rotation_ref, table_ref, q, keep)
 
+    copies[-1].wait()
     real, imag = evens(amps_ref)
     norm = jnp.sum(real * real + imag * imag)
     real, imag = turned(*looked_up(steps), real, imag)
@@ -353,18 +373,15 @@
     real, imag = turned(*looked_up(steps), real, imag)
     bits = []
     for b in range(plan.global_bits):
-        bits.append((b, *pair(1, ranked[b], (b >= late) & (b < slots))))
-    real, imag = by_blocks(split(gate(bits, plan.blocks)), real, imag)
-    pairs = []
-    for q in range(LANE_BITS):
-        keep = q == plan_ref[0, LANEQ]
-        for i in range(1, SWAPS):
-            keep = keep | (q == plan_ref[0, LANEQ + i])
-        pairs.append(pair(1, q, keep))
-    real, imag = by_lanes(split(gate(lane_bits(pairs), LANES)), real, imag)
+        leaving, i = ranked[b], plan.global_bits - 1 - b
+        if i < SWAPS:
+            leaving = jnp.where(b >= slots, plan_ref[0, LANEQ + i], leaving)
+        bits.append((b, *pair(1, leaving, b >= late)))
+    leave_gate = split(gate(bits, plan.blocks))
     buffer[...] = jnp.concatenate([real, imag], axis=0)
     swap(buffer, plan_ref, plan.global_bits)
-    put_blocks(out_ref, plan.blocks, 2 * plan.kept, plan.kept, buffer[:rows], buffer[rows:])
+    real, imag = by_blocks(leave_gate, buffer[:rows], buffer[rows:])
+    put_blocks(out_ref, plan.blocks, 2 * plan.kept, plan.kept, real, imag)
 
 
 def prepare_kernel(
@@ -503,6 +520,24 @@
     )(*scalars, *arrays)
 
 
+def first_call(plan, rotation, chain, coupling, bond, state):
+    sources = (rotation, chain, chain, coupling, bond, state)
+    spaces = (pltpu.SMEM,) * 2 + (pltpu.VMEM,) * 4
+    outs = (pltpu.VMEM, pltpu.VMEM, pltpu.SMEM)
+    return pl.pallas_call(
+        lambda *refs: first_kernel(plan, *refs),
+        out_shape=(
+            pltpu.VMEM(state.shape, F32), pltpu.VMEM((1, LANES), F32), pltpu.SMEM((1, PLAN), jnp.int32),
+        ),
+        in_specs=[spec(pl.ANY)] * len(sources),
+        out_specs=tuple(spec(s) for s in outs),
+        scratch_shapes=[pltpu.VMEM(state.shape, F32)]
+        + [space(a.shape, a.dtype) for space, a in zip(spaces, sources)]
+        + [pltpu.SMEM((2, ANGLES), F32), pltpu.SemaphoreType.DMA((len(sources),))],
+        name="first",
+    )(*sources)
+
+
 def local(amplitudes, coupling_index, rotation_index, chain_order, bond_sign):
     local_bits = amplitudes.shape[1].bit_length() - 1
     size = lax.axis_size("amp")
@@ -520,12 +555,7 @@
     square_of = lambda n: shape((n, n), BF16)
     buffer = (pltpu.VMEM((2 * rows, LANES), F32),)
 
-    state, sums, chosen = call(
-        bind(first_kernel),
-        (whole, line, shape((1, PLAN), jnp.int32)),
-        (rotation_index, table, chain), (*small, state), "first",
-        (pltpu.VMEM, pltpu.VMEM, pltpu.SMEM), buffer, held=(0, 1, 2),
-    )
+    state, sums, chosen = first_call(plan, rotation_index, chain, coupling_index, bond, state)
     sizes = (size, rows, LANES, rows)
     made = call(
         bind(prepare_kernel),

time: 51.9 us -> 51.7 us (level)
    pallas_call x4 -> x3, Pallas kernels: 7.73 us -> 4.15 us  [call(): pl.pallas_call(kernel, out_shape=shapes, in_specs=[spec(pltpu.SMEM)] * le...]
    pallas_call x0 -> x1, Pallas kernels: none -> 3.38 us  [first_call(): pl.pallas_call(lambda *refs: first_kernel(plan, *refs), out_shape=(pltpu....]
where the time goes in v1:
time: 51.7 us; the launch traced here: 51.5 us
  blocking collectives  18 us (35%)
  starting transfers between devices  15.4 us (30%)
  waiting for transfers between devices  9.2 us (18%)
  Pallas kernels  7.53 us (15%)
  between operations  1.3 us (3%)
    all_to_all x1, blocking collectives, end(): lax.all_to_all(state.reshape(size, height, 1, LANES), 'amp', 0, 0, tiled=...  18 us
    all_to_all x1, starting transfers between devices, local(): lax.all_to_all(state.reshape(size, 2 * plan.kept, LANES), 'amp', 0, 0, ti...  15.4 us
    all_to_all x1, waiting for transfers between devices, local(): lax.all_to_all(state.reshape(size, 2 * plan.kept, LANES), 'amp', 0, 0, ti...  9.2 us
    pallas_call x3, Pallas kernels, call(): pl.pallas_call(kernel, out_shape=shapes, in_specs=[spec(pltpu.SMEM)] * le...  4.15 us
    pallas_call x1, Pallas kernels, first_call(): pl.pallas_call(lambda *refs: first_kernel(plan, *refs), out_shape=(pltpu....  3.38 us
  transfers between devices with their start and end apart: 1, of which 1 were waited for; matrix products, arithmetic and copies ran while one was open for 0% of the time, Pallas kernels for 3%

profile of v1, /device:TPU:1, one launch (start us, length us, event | category | flops | bytes accessed | tf_op | source)
XLA Modules:
  0.0 51.5 jit_solution(10708449211323400990)
XLA Ops:
  0.6 3.4 %first.1 = (f32[512,128]{1,0:T(8,128)}, f32[1,128]{1,0:T(1,128)S(1)}, s32[1,16]{1,0:T(1,128)S(4)}) custom-call(s32[2,21]{1,0:T(2,128)} %refs_0_.3, s32[1,21]{1,0:T(1,128)} %bitcast.45, s32[1,21]{1,0:T(1,128)} %bitcast.46, s32[2,20]{1,0:T(2,128)} %refs_4_.1, s32[1,20]{1,0:T(1,128)} %bitcast.48, f32[512,128]{1,0:T(8,128)} %bitcast.44), custom_call_target="tpu_custom_call" | custom-call | tf_op jit(solution)/shard_map/first/pallas_call | solution.py:527
  4.0 15.4 %all-to-all-start.4 = ((f32[64,8,128]{2,1,0:T(8,128)}), f32[64,8,128]{2,1,0:T(8,128)S(1)}, u32[]{:S(2)}, u32[]{:S(2)}) async-start(f32[64,8,128]{2,1,0:T(8,128)} %bitcast.29), calls=%async_computation.4 | async-start | bytes 524288 | tf_op jit(solution)/shard_map/all_to_all | solution.py:568
  19.4 1.7 %prepare.1 = (s32[1,1]{1,0:T(1,128)}, f32[256,128]{1,0:T(8,128)S(1)}, f32[256,128]{1,0:T(8,128)S(1)}, f32[256,128]{1,0:T(8,128)S(1)}, f32[256,128]{1,0:T(8,128)S...) custom-call(s32[2,21]{1,0:T(2,128)} %refs_0_.3, ...), custom_call_target="tpu_custom_call" | custom-call | tf_op jit(solution)/shard_map/prepare/pallas_call | solution.py:513
  21.8 9.2 %all-to-all-done.4 = f32[64,8,128]{2,1,0:T(8,128)S(1)} async-done(((f32[64,8,128]{2,1,0:T(8,128)}), f32[64,8,128]{2,1,0:T(8,128)S(1)}, u32[]{:S(2)}, u32[]{:S(2)}) %all-to-all-start.4) | async-done | bytes 262176 | tf_op jit(solution)/shard_map/all_to_all | solution.py:568
  31.0 20.5 %conditional.1 = (f32[1,2]{1,0:T(1,128)}, f32[2,32768]{1,0:T(2,128)}) conditional(s32[]{:T(128)} %bitcast.28, (f32[512,128]{1,0:T(8,128)S(1)}, f32[256,128]{1,0:T(8,128)S(1)}, f32[256,128]{1,0:T(8,128)S(1)}, f32[256,128]{1,0:T(8,128)S(1)}, f32[256,128]{1,0:T(8,128)S(1)}, /*index=5*/f32[1,128]{1,0:T(1,128)S(1)}, ...), branch_computations={%region_0.0_spmd, %region_1.0_spmd, %region_2.0_spmd} | conditional | flops 128 | bytes 1638456 | solution.py:618
  31.0 1.0 %middle.2 = f32[576,128]{1,0:T(8,128)S(1)} custom-call(f32[512,128]{1,0:T(8,128)S(1)} %get-tuple-element.95.refs_0_, f32[256,128]{1,0:T(8,128)S(1)} %get-tuple-element.96.refs_1_, f32[256,128]{1,0:T(8,128)S(1)} %get-tuple-element.97.refs_2_, f32[256,128]{1,0:T(8,128)S(1)} %get-tuple-element.98.refs_3_, f32[256,128]{1,0:T(8,128)S(1)} %get-tuple-element.99.refs_4_, ...), custom_call_target="tpu_custom_call" | custom-call | tf_op jit(solution)/shard_map/cond/branch_0_fun/middle/pallas_call | solution.py:513
  32.0 18.0 %all_to_all.21 = f32[64,9,1,128]{3,2,1,0:T(1,128)S(1)} all-to-all(f32[64,9,1,128]{3,2,1,0:T(1,128)S(1)} %bitcast.42), channel_id=1, replica_groups=mesh['rep'=8,'amp'=64] {'amp'}, dimensions={0} | all-to-all | bytes 589824 | tf_op jit(solution)/shard_map/cond/branch_0_fun/all_to_all | solution.py:594
  50.0 1.5 %last.3 = (f32[512,128]{1,0:T(8,128)}, f32[1,2]{1,0:T(1,128)}) custom-call(s32[1,16]{1,0:T(1,128)S(4)} %get-tuple-element.94.refs_0_, f32[576,128]{1,0:T(8,128)S(1)} %bitcast.38, bf16[256,256]{1,0:T(8,128)(2,1)S(1)} %get-tuple-element.107.refs_2_, bf16[256,256]{1,0:T(8,128)(2,1)S(1)} %get-tuple-element.108.refs_3_), custom_call_target="tpu_custom_call" | custom-call | tf_op jit(solution)/shard_map/cond/branch_0_fun/last/pallas_call | solution.py:513
Async XLA Ops:
  4.0 26.9 %all-to-all-start.4 = ((f32[64,8,128]{2,1,0:T(8,128)}), f32[64,8,128]{2,1,0:T(8,128)S(1)}, u32[]{:S(2)}, u32[]{:S(2)}) async-start(f32[64,8,128]{2,1,0:T(8,128)} %bitcast.29), calls=%async_computation.4 | async-start | bytes 524288 | tf_op jit(solution)/shard_map/all_to_all | solution.py:568

commit v2 on v1

--- a/solution.py
+++ b/solution.py
@@ -152,7 +152,8 @@
 
 
 def energy(real, imag, field):
-    return jnp.sum((real * real + imag * imag) * field)
+    values = jnp.sum(((real * real + imag * imag) * field).reshape(-1, 8, LANES), axis=0)
+    return jnp.sum(jnp.sum(values, axis=0, keepdims=True), axis=1, keepdims=True)
 
 
 def in_lanes(parts):
@@ -204,39 +205,37 @@
     return both[:rows], both[rows:]
 
 
-def across(values, step):
-    place = iota((8, LANES), 1) ^ step
-    return jnp.concatenate(
-        [
-            jnp.take_along_axis(values[k : k + 8], place, axis=1, mode="promise_in_bounds")
-            for k in range(0, values.shape[0], 8)
-        ],
-        axis=0,
-    )
-
-
-def swap(buffer, plan_ref, slots):
+def swap(plan, load, buffer, plan_ref):
+    tiles = plan.blocks // 8
+    top = tiles.bit_length() - 2
+    lane, row = iota((8, LANES), 1), iota((8, LANES), 0)
+    steps = []
     for i in range(SWAPS):
-        @pl.when(i < plan_ref[0, SWAPPED])
-        def _(i=i):
-            height = 2 ** (slots - 1 - i)
-            place = plan_ref[0, LANEQ + i]
-            step = jnp.left_shift(jnp.int32(1), place)
-            if height == 4:
-                tiles = buffer[...].reshape(-1, 8, LANES)
-                other = pltpu.roll(tiles, 4, 1)
-                one = (iota((1, 8, LANES), 2) >> place) & 1
-                same = one == (iota((1, 8, LANES), 1) >> 2)
-                moved = across(other.reshape(-1, LANES), step).reshape(tiles.shape)
-                buffer[...] = jnp.where(same, tiles, moved).reshape(buffer.shape)
-                return
-            whole = buffer[...].reshape(-1, 2, height, LANES)
-            low, high = whole[:, 0].reshape(-1, LANES), whole[:, 1].reshape(-1, LANES)
-            one = ((iota((1, LANES), 1) >> place) & 1) == 1
-            crossed = across(jnp.where(one, low, high), step)
-            new_low, new_high = jnp.where(one, crossed, low), jnp.where(one, high, crossed)
-            pairs = (new_low.reshape(-1, 1, height, LANES), new_high.reshape(-1, 1, height, LANES))
-            buffer[...] = jnp.concatenate(pairs, axis=1).reshape(buffer.shape)
+        taken = i < plan_ref[0, SWAPPED]
+        steps.append(jnp.where(taken, jnp.left_shift(jnp.int32(1), plan_ref[0, LANEQ + i] & 7), 0))
+    ones = [(lane & step) != 0 for step in steps]
+    places = [lane ^ step for step in steps]
+    cross = lambda value, i: jnp.take_along_axis(value, places[i], axis=1, mode="promise_in_bounds")
+    for part in range(2 * plan.kept):
+        values = [load(part, at) for at in range(tiles)]
+        for i in range(top + 1):
+            bit = 1 << (top - i)
+            for low in range(tiles):
+                if low & bit:
+                    continue
+                first, second = values[low], values[low | bit]
+                crossed = cross(jnp.where(ones[i], first, second), i)
+                values[low] = jnp.where(ones[i], crossed, first)
+                values[low | bit] = jnp.where(ones[i], second, crossed)
+        for at in range(tiles):
+            buffer[pl.ds(part * plan.blocks + at * 8, 8), :] = values[at]
+
+    @pl.when(plan_ref[0, SWAPPED] > top + 1)
+    def _():
+        same = ones[top + 1] == ((row & 4) != 0)
+        for at in range(0, buffer.shape[0], 8):
+            value = buffer[pl.ds(at, 8), :]
+            buffer[pl.ds(at, 8), :] = jnp.where(same, value, cross(pltpu.roll(value, 4, 0), top + 1))
 
 
 class Plan:
@@ -354,7 +353,7 @@
 
     copies[-1].wait()
     real, imag = evens(amps_ref)
-    norm = jnp.sum(real * real + imag * imag)
+    norm = energy(real, imag, 1.0)
     real, imag = turned(*looked_up(steps), real, imag)
     ranked = [plan_ref[0, ROWQ + b] for b in range(plan.row_bits)]
     row_gate = gate([(q - LANE_BITS, *pair(0, q)) for q in ranked], rows)
@@ -378,8 +377,9 @@
             leaving = jnp.where(b >= slots, plan_ref[0, LANEQ + i], leaving)
         bits.append((b, *pair(1, leaving, b >= late)))
     leave_gate = split(gate(bits, plan.blocks))
-    buffer[...] = jnp.concatenate([real, imag], axis=0)
-    swap(buffer, plan_ref, plan.global_bits)
+    whole = jnp.concatenate([real, imag], axis=0)
+    held_tile = lambda part, at: whole[part * plan.blocks + at * 8 :][:8]
+    swap(plan, held_tile, buffer, plan_ref)
     real, imag = by_blocks(leave_gate, buffer[:rows], buffer[rows:])
     put_blocks(out_ref, plan.blocks, 2 * plan.kept, plan.kept, real, imag)
 
@@ -478,9 +478,12 @@
     factor = 1.0 / jnp.sqrt(mean)
     square = factor * factor / amps
     energies_ref[...] = sums[:, 1 : 1 + LAYERS] * square
-    real, imag = take_blocks(state_ref, blocks, height, kept)
-    buffer[...] = jnp.concatenate([real, imag], axis=0)
-    swap(buffer, plan_ref, plan.global_bits)
+
+    def came(part, at):
+        component, k = divmod(part, kept)
+        return state_ref[pl.ds(2 * k + component + 8 * height * at, 8, stride=height), :]
+
+    swap(plan, came, buffer, plan_ref)
     real, imag = by_rows((ga[...], gb[...]), buffer[:rows], buffer[rows:])
     if late_ref:
         late_out_ref[0][...] = in_lanes([0.0, energy(real, imag, late_ref[0][...])])[:, 0:LAYERS] * square

time: 51.7 us -> 51.2 us (level)
  Pallas kernels: 7.53 us -> 7 us
where the time goes in v2:
time: 51.2 us; the launch traced here: 50.9 us
  blocking collectives  18 us (35%)
  starting transfers between devices  15.4 us (30%)
  waiting for transfers between devices  9.2 us (18%)
  Pallas kernels  7 us (14%)
  between operations  1.3 us (3%)
    all_to_all x1, blocking collectives, end(): lax.all_to_all(state.reshape(size, height, 1, LANES), 'amp', 0, 0, tiled=...  18 us
    all_to_all x1, starting transfers between devices, local(): lax.all_to_all(state.reshape(size, 2 * plan.kept, LANES), 'amp', 0, 0, ti...  15.4 us
    all_to_all x1, waiting for transfers between devices, local(): lax.all_to_all(state.reshape(size, 2 * plan.kept, LANES), 'amp', 0, 0, ti...  9.2 us
    pallas_call x3, Pallas kernels, call(): pl.pallas_call(kernel, out_shape=shapes, in_specs=[spec(pltpu.SMEM)] * le...  3.86 us
    pallas_call x1, Pallas kernels, first_call(): pl.pallas_call(lambda *refs: first_kernel(plan, *refs), out_shape=(pltpu....  3.14 us
  transfers between devices with their start and end apart: 1, of which 1 were waited for; matrix products, arithmetic and copies ran while one was open for 0% of the time, Pallas kernels for 3%

profile of v2, /device:TPU:1, one launch (start us, length us, event | category | flops | bytes accessed | tf_op | source)
XLA Modules:
  0.0 50.9 jit_solution(659311660927189735)
XLA Ops:
  0.6 3.1 %first.1 = (f32[512,128]{1,0:T(8,128)}, f32[1,128]{1,0:T(1,128)S(1)}, s32[1,16]{1,0:T(1,128)S(4)}) custom-call(s32[2,21]{1,0:T(2,128)} %refs_0_.3, s32[1,21]{1,0:T(1,128)} %bitcast.45, s32[1,21]{1,0:T(1,128)} %bitcast.46, s32[2,20]{1,0:T(2,128)} %refs_4_.1, s32[1,20]{1,0:T(1,128)} %bitcast.48, f32[512,128]{1,0:T(8,128)} %bitcast.44), custom_call_target="tpu_custom_call" | custom-call | tf_op jit(solution)/shard_map/first/pallas_call | solution.py:530
  3.8 15.4 %all-to-all-start.4 = ((f32[64,8,128]{2,1,0:T(8,128)}), f32[64,8,128]{2,1,0:T(8,128)S(1)}, u32[]{:S(2)}, u32[]{:S(2)}) async-start(f32[64,8,128]{2,1,0:T(8,128)} %bitcast.29), calls=%async_computation.4 | async-start | bytes 524288 | tf_op jit(solution)/shard_map/all_to_all | solution.py:571
  19.2 1.7 %prepare.1 = (s32[1,1]{1,0:T(1,128)}, f32[256,128]{1,0:T(8,128)S(1)}, f32[256,128]{1,0:T(8,128)S(1)}, f32[256,128]{1,0:T(8,128)S(1)}, f32[256,128]{1,0:T(8,128)S...) custom-call(s32[2,21]{1,0:T(2,128)} %refs_0_.3, ...), custom_call_target="tpu_custom_call" | custom-call | tf_op jit(solution)/shard_map/prepare/pallas_call | solution.py:516
  21.5 9.2 %all-to-all-done.4 = f32[64,8,128]{2,1,0:T(8,128)S(1)} async-done(((f32[64,8,128]{2,1,0:T(8,128)}), f32[64,8,128]{2,1,0:T(8,128)S(1)}, u32[]{:S(2)}, u32[]{:S(2)}) %all-to-all-start.4) | async-done | bytes 262176 | tf_op jit(solution)/shard_map/all_to_all | solution.py:571
  30.7 20.2 %conditional.1 = (f32[1,2]{1,0:T(1,128)}, f32[2,32768]{1,0:T(2,128)}) conditional(s32[]{:T(128)} %bitcast.28, (f32[512,128]{1,0:T(8,128)S(1)}, f32[256,128]{1,0:T(8,128)S(1)}, f32[256,128]{1,0:T(8,128)S(1)}, f32[256,128]{1,0:T(8,128)S(1)}, f32[256,128]{1,0:T(8,128)S(1)}, /*index=5*/f32[1,128]{1,0:T(1,128)S(1)}, ...), branch_computations={%region_0.0_spmd, %region_1.0_spmd, %region_2.0_spmd} | conditional | flops 128 | bytes 1638456 | solution.py:621
  30.7 1.0 %middle.2 = f32[576,128]{1,0:T(8,128)S(1)} custom-call(f32[512,128]{1,0:T(8,128)S(1)} %get-tuple-element.95.refs_0_, f32[256,128]{1,0:T(8,128)S(1)} %get-tuple-element.96.refs_1_, f32[256,128]{1,0:T(8,128)S(1)} %get-tuple-element.97.refs_2_, f32[256,128]{1,0:T(8,128)S(1)} %get-tuple-element.98.refs_3_, f32[256,128]{1,0:T(8,128)S(1)} %get-tuple-element.99.refs_4_, ...), custom_call_target="tpu_custom_call" | custom-call | tf_op jit(solution)/shard_map/cond/branch_0_fun/middle/pallas_call | solution.py:516
  31.7 18.0 %all_to_all.21 = f32[64,9,1,128]{3,2,1,0:T(1,128)S(1)} all-to-all(f32[64,9,1,128]{3,2,1,0:T(1,128)S(1)} %bitcast.42), channel_id=1, replica_groups=mesh['rep'=8,'amp'=64] {'amp'}, dimensions={0} | all-to-all | bytes 589824 | tf_op jit(solution)/shard_map/cond/branch_0_fun/all_to_all | solution.py:597
  49.7 1.2 %last.3 = (f32[512,128]{1,0:T(8,128)}, f32[1,2]{1,0:T(1,128)}) custom-call(s32[1,16]{1,0:T(1,128)S(4)} %get-tuple-element.94.refs_0_, f32[576,128]{1,0:T(8,128)S(1)} %bitcast.38, bf16[256,256]{1,0:T(8,128)(2,1)S(1)} %get-tuple-element.107.refs_2_, bf16[256,256]{1,0:T(8,128)(2,1)S(1)} %get-tuple-element.108.refs_3_), custom_call_target="tpu_custom_call" | custom-call | tf_op jit(solution)/shard_map/cond/branch_0_fun/last/pallas_call | solution.py:516
Async XLA Ops:
  3.8 26.9 %all-to-all-start.4 = ((f32[64,8,128]{2,1,0:T(8,128)}), f32[64,8,128]{2,1,0:T(8,128)S(1)}, u32[]{:S(2)}, u32[]{:S(2)}) async-start(f32[64,8,128]{2,1,0:T(8,128)} %bitcast.29), calls=%async_computation.4 | async-start | bytes 524288 | tf_op jit(solution)/shard_map/all_to_all | solution.py:571

commit v3 on v2

--- a/solution.py
+++ b/solution.py
@@ -319,10 +319,13 @@
     return places
 
 
-def row_ones(plan, device):
+def tile_ones(plan, device):
     tile = bit_count(iota((8, LANES), 0), 3) + bit_count(iota((8, LANES), 1), LANE_BITS)
-    tile = tile + bit_count(device, plan.global_bits)
-    return jnp.concatenate([tile + k.bit_count() for k in range(plan.rows // 8)], axis=0)
+    return tile + bit_count(device, plan.global_bits)
+
+
+def per_tile(plan, tiles):
+    return jnp.concatenate([tiles[k.bit_count() % len(tiles)] for k in range(plan.rows // 8)], axis=0)
 
 
 def first_kernel(plan, *refs):
@@ -348,7 +351,8 @@
         [(coupling_ref[0:1, :] + 1).astype(F32) * bond_signs],
         chain, lanes, device_bits, bonds, plan.row_bits,
     )
-    steps = steps + (UNITS // 2) * row_ones(plan, device).astype(F32)
+    ones = (UNITS // 2) * tile_ones(plan, device).astype(F32)
+    steps = steps + per_tile(plan, [ones + (UNITS // 2) * k for k in range(4)])
     pair = lambda layer, q, keep=None: pair_of(layer, rotation_ref, table_ref, q, keep)
 
     copies[-1].wait()
@@ -487,11 +491,13 @@
     real, imag = by_rows((ga[...], gb[...]), buffer[:rows], buffer[rows:])
     if late_ref:
         late_out_ref[0][...] = in_lanes([0.0, energy(real, imag, late_ref[0][...])])[:, 0:LAYERS] * square
-    ones = row_ones(plan, device)
+    ones = tile_ones(plan, device)
+    scale = jnp.where(((ones + 1) & 2) == 2, -factor, factor)
     odd = (ones & 1) == 1
-    real, imag = jnp.where(odd, imag, real), jnp.where(odd, real, imag)
-    real = jnp.where(((ones + 1) & 2) == 2, -factor, factor) * real
-    imag = jnp.where((ones & 2) == 2, -factor, factor) * imag
+    same, other = jnp.where(odd, 0.0, scale), jnp.where(odd, scale, 0.0)
+    cosine = per_tile(plan, [same, other, -same, -other])
+    sine = per_tile(plan, [other, -same, -other, same])
+    real, imag = turned(cosine, sine, real, imag)
     out_ref[pl.ds(0, rows, stride=2), :] = real
     out_ref[pl.ds(1, rows, stride=2), :] = imag
 

time: 51.2 us -> 51.3 us (level)
  no operation moved by 1% of the time
where the time goes in v3:
time: 51.3 us; the launch traced here: 50.9 us
  blocking collectives  18 us (35%)
  starting transfers between devices  15.4 us (30%)
  waiting for transfers between devices  9.2 us (18%)
  Pallas kernels  7 us (14%)
  between operations  1.3 us (3%)
    all_to_all x1, blocking collectives, end(): lax.all_to_all(state.reshape(size, height, 1, LANES), 'amp', 0, 0, tiled=...  18 us
    all_to_all x1, starting transfers between devices, local(): lax.all_to_all(state.reshape(size, 2 * plan.kept, LANES), 'amp', 0, 0, ti...  15.4 us
    all_to_all x1, waiting for transfers between devices, local(): lax.all_to_all(state.reshape(size, 2 * plan.kept, LANES), 'amp', 0, 0, ti...  9.2 us
    pallas_call x3, Pallas kernels, call(): pl.pallas_call(kernel, out_shape=shapes, in_specs=[spec(pltpu.SMEM)] * le...  3.86 us
    pallas_call x1, Pallas kernels, first_call(): pl.pallas_call(lambda *refs: first_kernel(plan, *refs), out_shape=(pltpu....  3.14 us
  transfers between devices with their start and end apart: 1, of which 1 were waited for; matrix products, arithmetic and copies ran while one was open for 0% of the time, Pallas kernels for 3%

profile of v3, /device:TPU:1, one launch (start us, length us, event | category | flops | bytes accessed | tf_op | source)
XLA Modules:
  0.0 50.9 jit_solution(6533012534062119259)
XLA Ops:
  0.6 3.1 %first.1 = (f32[512,128]{1,0:T(8,128)}, f32[1,128]{1,0:T(1,128)S(1)}, s32[1,16]{1,0:T(1,128)S(4)}) custom-call(s32[2,21]{1,0:T(2,128)} %refs_0_.3, s32[1,21]{1,0:T(1,128)} %bitcast.45, s32[1,21]{1,0:T(1,128)} %bitcast.46, s32[2,20]{1,0:T(2,128)} %refs_4_.1, s32[1,20]{1,0:T(1,128)} %bitcast.48, f32[512,128]{1,0:T(8,128)} %bitcast.44), custom_call_target="tpu_custom_call" | custom-call | tf_op jit(solution)/shard_map/first/pallas_call | solution.py:536
  3.8 15.4 %all-to-all-start.4 = ((f32[64,8,128]{2,1,0:T(8,128)}), f32[64,8,128]{2,1,0:T(8,128)S(1)}, u32[]{:S(2)}, u32[]{:S(2)}) async-start(f32[64,8,128]{2,1,0:T(8,128)} %bitcast.29), calls=%async_computation.4 | async-start | bytes 524288 | tf_op jit(solution)/shard_map/all_to_all | solution.py:577
  19.2 1.7 %prepare.1 = (s32[1,1]{1,0:T(1,128)}, f32[256,128]{1,0:T(8,128)S(1)}, f32[256,128]{1,0:T(8,128)S(1)}, f32[256,128]{1,0:T(8,128)S(1)}, f32[256,128]{1,0:T(8,128)S...) custom-call(s32[2,21]{1,0:T(2,128)} %refs_0_.3, ...), custom_call_target="tpu_custom_call" | custom-call | tf_op jit(solution)/shard_map/prepare/pallas_call | solution.py:522
  21.5 9.2 %all-to-all-done.4 = f32[64,8,128]{2,1,0:T(8,128)S(1)} async-done(((f32[64,8,128]{2,1,0:T(8,128)}), f32[64,8,128]{2,1,0:T(8,128)S(1)}, u32[]{:S(2)}, u32[]{:S(2)}) %all-to-all-start.4) | async-done | bytes 262176 | tf_op jit(solution)/shard_map/all_to_all | solution.py:577
  30.7 20.2 %conditional.1 = (f32[1,2]{1,0:T(1,128)}, f32[2,32768]{1,0:T(2,128)}) conditional(s32[]{:T(128)} %bitcast.28, (f32[512,128]{1,0:T(8,128)S(1)}, f32[256,128]{1,0:T(8,128)S(1)}, f32[256,128]{1,0:T(8,128)S(1)}, f32[256,128]{1,0:T(8,128)S(1)}, f32[256,128]{1,0:T(8,128)S(1)}, /*index=5*/f32[1,128]{1,0:T(1,128)S(1)}, ...), branch_computations={%region_0.0_spmd, %region_1.0_spmd, %region_2.0_spmd} | conditional | flops 128 | bytes 1638456 | solution.py:627
  30.7 1.0 %middle.2 = f32[576,128]{1,0:T(8,128)S(1)} custom-call(f32[512,128]{1,0:T(8,128)S(1)} %get-tuple-element.95.refs_0_, f32[256,128]{1,0:T(8,128)S(1)} %get-tuple-element.96.refs_1_, f32[256,128]{1,0:T(8,128)S(1)} %get-tuple-element.97.refs_2_, f32[256,128]{1,0:T(8,128)S(1)} %get-tuple-element.98.refs_3_, f32[256,128]{1,0:T(8,128)S(1)} %get-tuple-element.99.refs_4_, ...), custom_call_target="tpu_custom_call" | custom-call | tf_op jit(solution)/shard_map/cond/branch_0_fun/middle/pallas_call | solution.py:522
  31.7 18.0 %all_to_all.21 = f32[64,9,1,128]{3,2,1,0:T(1,128)S(1)} all-to-all(f32[64,9,1,128]{3,2,1,0:T(1,128)S(1)} %bitcast.42), channel_id=1, replica_groups=mesh['rep'=8,'amp'=64] {'amp'}, dimensions={0} | all-to-all | bytes 589824 | tf_op jit(solution)/shard_map/cond/branch_0_fun/all_to_all | solution.py:603
  49.7 1.2 %last.3 = (f32[512,128]{1,0:T(8,128)}, f32[1,2]{1,0:T(1,128)}) custom-call(s32[1,16]{1,0:T(1,128)S(4)} %get-tuple-element.94.refs_0_, f32[576,128]{1,0:T(8,128)S(1)} %bitcast.38, bf16[256,256]{1,0:T(8,128)(2,1)S(1)} %get-tuple-element.107.refs_2_, bf16[256,256]{1,0:T(8,128)(2,1)S(1)} %get-tuple-element.108.refs_3_), custom_call_target="tpu_custom_call" | custom-call | tf_op jit(solution)/shard_map/cond/branch_0_fun/last/pallas_call | solution.py:522
Async XLA Ops:
  3.8 26.9 %all-to-all-start.4 = ((f32[64,8,128]{2,1,0:T(8,128)}), f32[64,8,128]{2,1,0:T(8,128)S(1)}, u32[]{:S(2)}, u32[]{:S(2)}) async-start(f32[64,8,128]{2,1,0:T(8,128)} %bitcast.29), calls=%async_computation.4 | async-start | bytes 524288 | tf_op jit(solution)/shard_map/all_to_all | solution.py:577

commit v4 on v3

--- a/solution.py
+++ b/solution.py
@@ -342,7 +342,6 @@
     rotation_ref, order_ref, chain_ref, coupling_ref, bond_ref, amps_ref = held
     device = lax.axis_index("amp")
     bonds, rows = plan.bonds, plan.rows
-    choose(plan, order_ref, plan_ref)
     chain = chain_ref[...]
     device_bits = device << plan.local_bits
     bond_signs = (2 * bond_ref[...] - 1).astype(F32)
@@ -355,6 +354,7 @@
     steps = steps + per_tile(plan, [ones + (UNITS // 2) * k for k in range(4)])
     pair = lambda layer, q, keep=None: pair_of(layer, rotation_ref, table_ref, q, keep)
 
+    choose(plan, order_ref, plan_ref)
     copies[-1].wait()
     real, imag = evens(amps_ref)
     norm = energy(real, imag, 1.0)

time: 51.3 us -> 51.2 us (level)
  no operation moved by 1% of the time
where the time goes in v4:
time: 51.2 us; the launch traced here: 50.9 us
  blocking collectives  18 us (35%)
  starting transfers between devices  15.4 us (30%)
  waiting for transfers between devices  9.2 us (18%)
  Pallas kernels  7 us (14%)
  between operations  1.3 us (3%)
    all_to_all x1, blocking collectives, end(): lax.all_to_all(state.reshape(size, height, 1, LANES), 'amp', 0, 0, tiled=...  18 us
    all_to_all x1, starting transfers between devices, local(): lax.all_to_all(state.reshape(size, 2 * plan.kept, LANES), 'amp', 0, 0, ti...  15.4 us
    all_to_all x1, waiting for transfers between devices, local(): lax.all_to_all(state.reshape(size, 2 * plan.kept, LANES), 'amp', 0, 0, ti...  9.2 us
    pallas_call x3, Pallas kernels, call(): pl.pallas_call(kernel, out_shape=shapes, in_specs=[spec(pltpu.SMEM)] * le...  3.86 us
    pallas_call x1, Pallas kernels, first_call(): pl.pallas_call(lambda *refs: first_kernel(plan, *refs), out_shape=(pltpu....  3.14 us
  transfers between devices with their start and end apart: 1, of which 1 were waited for; matrix products, arithmetic and copies ran while one was open for 0% of the time, Pallas kernels for 3%

profile of v4, /device:TPU:1, one launch (start us, length us, event | category | flops | bytes accessed | tf_op | source)
XLA Modules:
  0.0 50.9 jit_solution(6533012534062119259)
XLA Ops:
  0.6 3.1 %first.1 = (f32[512,128]{1,0:T(8,128)}, f32[1,128]{1,0:T(1,128)S(1)}, s32[1,16]{1,0:T(1,128)S(4)}) custom-call(s32[2,21]{1,0:T(2,128)} %refs_0_.3, s32[1,21]{1,0:T(1,128)} %bitcast.45, s32[1,21]{1,0:T(1,128)} %bitcast.46, s32[2,20]{1,0:T(2,128)} %refs_4_.1, s32[1,20]{1,0:T(1,128)} %bitcast.48, f32[512,128]{1,0:T(8,128)} %bitcast.44), custom_call_target="tpu_custom_call" | custom-call | tf_op jit(solution)/shard_map/first/pallas_call | solution.py:536
  3.8 15.4 %all-to-all-start.4 = ((f32[64,8,128]{2,1,0:T(8,128)}), f32[64,8,128]{2,1,0:T(8,128)S(1)}, u32[]{:S(2)}, u32[]{:S(2)}) async-start(f32[64,8,128]{2,1,0:T(8,128)} %bitcast.29), calls=%async_computation.4 | async-start | bytes 524288 | tf_op jit(solution)/shard_map/all_to_all | solution.py:577
  19.2 1.7 %prepare.1 = (s32[1,1]{1,0:T(1,128)}, f32[256,128]{1,0:T(8,128)S(1)}, f32[256,128]{1,0:T(8,128)S(1)}, f32[256,128]{1,0:T(8,128)S(1)}, f32[256,128]{1,0:T(8,128)S...) custom-call(s32[2,21]{1,0:T(2,128)} %refs_0_.3, ...), custom_call_target="tpu_custom_call" | custom-call | tf_op jit(solution)/shard_map/prepare/pallas_call | solution.py:522
  21.5 9.2 %all-to-all-done.4 = f32[64,8,128]{2,1,0:T(8,128)S(1)} async-done(((f32[64,8,128]{2,1,0:T(8,128)}), f32[64,8,128]{2,1,0:T(8,128)S(1)}, u32[]{:S(2)}, u32[]{:S(2)}) %all-to-all-start.4) | async-done | bytes 262176 | tf_op jit(solution)/shard_map/all_to_all | solution.py:577
  30.7 20.2 %conditional.1 = (f32[1,2]{1,0:T(1,128)}, f32[2,32768]{1,0:T(2,128)}) conditional(s32[]{:T(128)} %bitcast.28, (f32[512,128]{1,0:T(8,128)S(1)}, f32[256,128]{1,0:T(8,128)S(1)}, f32[256,128]{1,0:T(8,128)S(1)}, f32[256,128]{1,0:T(8,128)S(1)}, f32[256,128]{1,0:T(8,128)S(1)}, /*index=5*/f32[1,128]{1,0:T(1,128)S(1)}, ...), branch_computations={%region_0.0_spmd, %region_1.0_spmd, %region_2.0_spmd} | conditional | flops 128 | bytes 1638456 | solution.py:627
  30.7 1.0 %middle.2 = f32[576,128]{1,0:T(8,128)S(1)} custom-call(f32[512,128]{1,0:T(8,128)S(1)} %get-tuple-element.95.refs_0_, f32[256,128]{1,0:T(8,128)S(1)} %get-tuple-element.96.refs_1_, f32[256,128]{1,0:T(8,128)S(1)} %get-tuple-element.97.refs_2_, f32[256,128]{1,0:T(8,128)S(1)} %get-tuple-element.98.refs_3_, f32[256,128]{1,0:T(8,128)S(1)} %get-tuple-element.99.refs_4_, ...), custom_call_target="tpu_custom_call" | custom-call | tf_op jit(solution)/shard_map/cond/branch_0_fun/middle/pallas_call | solution.py:522
  31.7 18.0 %all_to_all.21 = f32[64,9,1,128]{3,2,1,0:T(1,128)S(1)} all-to-all(f32[64,9,1,128]{3,2,1,0:T(1,128)S(1)} %bitcast.42), channel_id=1, replica_groups=mesh['rep'=8,'amp'=64] {'amp'}, dimensions={0} | all-to-all | bytes 589824 | tf_op jit(solution)/shard_map/cond/branch_0_fun/all_to_all | solution.py:603
  49.7 1.2 %last.3 = (f32[512,128]{1,0:T(8,128)}, f32[1,2]{1,0:T(1,128)}) custom-call(s32[1,16]{1,0:T(1,128)S(4)} %get-tuple-element.94.refs_0_, f32[576,128]{1,0:T(8,128)S(1)} %bitcast.38, bf16[256,256]{1,0:T(8,128)(2,1)S(1)} %get-tuple-element.107.refs_2_, bf16[256,256]{1,0:T(8,128)(2,1)S(1)} %get-tuple-element.108.refs_3_), custom_call_target="tpu_custom_call" | custom-call | tf_op jit(solution)/shard_map/cond/branch_0_fun/last/pallas_call | solution.py:522
Async XLA Ops:
  3.8 26.9 %all-to-all-start.4 = ((f32[64,8,128]{2,1,0:T(8,128)}), f32[64,8,128]{2,1,0:T(8,128)S(1)}, u32[]{:S(2)}, u32[]{:S(2)}) async-start(f32[64,8,128]{2,1,0:T(8,128)} %bitcast.29), calls=%async_computation.4 | async-start | bytes 524288 | tf_op jit(solution)/shard_map/all_to_all | solution.py:577
